TPU v7x, 32 devices: a whole 2x2x4 slice. The times are simulated.
32 devices in a mesh: floor: 4 (over y, x), zone: 8 (over z, core).
Axes of the slice: x: 2, y: 2, z: 4, core: 2. Of those that a mesh axis runs over, the one named last changes fastest.
Arguments:
- factor: float32 [512, 96, 384], P(('floor', 'zone')), may hold values from -0.625 to 0.625
- plant_map: float32 [512, 96, 384], P(('floor', 'zone')), may hold values from -0.4082483 to 0.4082483
- offset: float32 [512, 384], P(('floor', 'zone')), may hold values from -10 to 10
- start_plan: float32 [512, 384], P(('floor', 'zone')), may hold values from -10 to 10
- demand: float32 [4, 48], replicated, may hold values from -768 to 768
- start_price: float32 [4, 48], replicated, may hold values from -6 to 6
- start_multiplier: float32 [512, 48], P(('floor', 'zone')), may hold values from -6 to 6
- neighbors: int32 [512, 4], P(('floor', 'zone')), may hold values from 0 to 127
- loop_of_zone: int32 [512], P(('floor', 'zone')), may hold values from 0 to 3
Outputs:
- control: float32 [512, 384], P(('floor', 'zone'))
- price: float32 [4, 48], replicated
- multiplier: float32 [512, 48], P(('floor', 'zone'))
Inputs may be any that keep to these rules, and one draw needn't show every extreme that they name: `neighbors`: indices count zones within the zone's own floor of 128 consecutive zones.
All inputs are finite; a program needn't handle non-finite values.
Results may differ from a plain program's by a relative error of at most 0.0001.
Values sent between devices are 32-bit elements; how exact they have to be, the bound alone decides.
No kernel may reach another device: no remote copies, remote signals or barrier semaphores. Data moves between devices by JAX's collectives and lax.ppermute only.
A program may use at most 64 MiB of HBM per device.

v0:
```python
import jax
import jax.numpy as jnp
from jax import lax
from jax.sharding import PartitionSpec as P

HORIZON = 48
NEIGHBORS = 4
LOOPS = 4
ITERS = 2


def select_rows(neighbors, count):
    columns = jnp.arange(count, dtype=jnp.int32)
    picks = (neighbors[:, :, None] == columns[None, None, :]).astype(jnp.float32)
    return jnp.sum(picks, axis=1) / NEIGHBORS


def local(
    factor,
    plant_map,
    offset,
    start_plan,
    demand,
    start_price,
    start_multiplier,
    neighbors,
    loop_of_zone,
):
    control = start_plan
    price = start_price
    multiplier = start_multiplier
    zones_here = control.shape[0]
    zones_all = zones_here * lax.axis_size("floor") * lax.axis_size("zone")
    onehot = (loop_of_zone[:, None] == jnp.arange(LOOPS, dtype=jnp.int32)[None, :]).astype(
        jnp.float32
    )
    for step in range(ITERS):
        outputs = jnp.einsum("zkv,zv->zk", plant_map, control, precision=lax.Precision.HIGHEST)
        shares = outputs[:, :HORIZON]
        bound = outputs[:, HORIZON:]
        partial_load = jnp.dot(onehot.T, shares, precision=lax.Precision.HIGHEST)
        floor_load = lax.psum(partial_load, "zone")
        total = lax.psum(floor_load, "floor")
        excess = (total - demand) * (LOOPS / zones_all)
        shift = jnp.dot(onehot, excess + price, precision=lax.Precision.HIGHEST)
        price = price + excess
        target_share = shares - shift
        floor_bound = lax.all_gather(bound, "zone", axis=0, tiled=True)
        weights = select_rows(neighbors, floor_bound.shape[0])
        near = jnp.dot(weights, floor_bound, precision=lax.Precision.HIGHEST)
        target_bound = (bound + near) / 2.0 - multiplier
        multiplier = multiplier + (bound - near) / 2.0
        target = jnp.concatenate([target_share, target_bound], axis=1)
        control = (
            0.8 * jnp.einsum("zkv,zk->zv", factor, target, precision=lax.Precision.HIGHEST) - offset
        )
    return (control, price, multiplier)


def solution(mesh):
    placed = (
        P(("floor", "zone"), None, None),
        P(("floor", "zone"), None, None),
        P(("floor", "zone"), None),
        P(("floor", "zone"), None),
        P(),
        P(),
        P(("floor", "zone"), None),
        P(("floor", "zone"), None),
        P(("floor", "zone")),
    )
    return jax.shard_map(
        local,
        mesh=mesh,
        in_specs=placed,
        out_specs=(P(("floor", "zone"), None), P(), P(("floor", "zone"), None)),
        check_vma=False,
    )
```

profile of v0, /device:TPU:0, one launch (start us, length us, event | category | flops | bytes accessed | tf_op | source)
XLA Modules:
  0.0 91.8 jit_solution(17976281189199001725)
XLA Ops:
  0.6 0.0 copy-start
  0.6 0.0 copy-start.3
  0.7 0.0 copy-start.4
  0.7 0.0 copy-start.8
  0.7 0.0 copy-start.5
  0.7 0.0 copy-start.6
  0.7 0.0 copy-start.2
  0.7 4.4 %fusion.5 = f32[16,1,96]{2,1,0:T(1,128)S(1)} fusion(f32[16,96,384]{2,1,0:T(8,128)} %param.10, f32[16,384,1]{1,0,2:T(8,128)} %bitcast.43), kind=kOutput, calls=%fused_computation.11 | convolution fusion | flops 7077888 | bytes 2390016 | tf_op jit(solution)/shard_map/zkv,zv->zk/dot_general | solution.py:38
  5.1 0.1 slice.17
  5.2 15.7 %all_gather.6 = f32[128,48]{1,0:T(8,128)S(1)} all-gather(f32[16,48]{1,0:T(8,128)S(1)} %slice.17), channel_id=1, replica_groups=mesh['floor'=4,'zone'=8] {'zone'}, dimensions={0}, use_global_device_ids=true | all-gather | bytes 27648 | tf_op jit(solution)/shard_map/all_gather | solution.py:48
  20.9 0.0 copy-done.4
  20.9 0.1 convert_reduce_fusion
  21.0 0.0 copy-done.3
  21.0 0.2 multiply_subtract_fusion.1
  21.1 0.0 copy-done.8
  21.1 0.3 fusion.8
  21.4 16.9 %psum.28 = f32[4,48]{1,0:T(4,128)S(1)} all-reduce(f32[4,48]{1,0:T(4,128)S(1)} %fusion.8), channel_id=1, replica_groups=mesh['floor'=4,'zone'=8] {'zone'}, use_global_device_ids=true, to_apply=%region_0.0 | all-reduce | flops 192 | bytes 1536 | tf_op jit(solution)/shard_map/psum | solution.py:42
  38.3 9.9 %psum.29 = f32[4,48]{1,0:T(4,128)S(1)} all-reduce(f32[4,48]{1,0:T(4,128)S(1)} %psum.28), channel_id=1, replica_groups=mesh['floor'=4,'zone'=8] {'floor'}, use_global_device_ids=true, to_apply=%region_1.0 | all-reduce | flops 192 | bytes 1536 | tf_op jit(solution)/shard_map/psum | solution.py:43
  48.2 0.0 copy-done.5
  48.2 0.0 copy-done.6
  48.2 0.0 copy-start.1
  48.2 0.2 convolution_subtract_fusion.1
  48.4 0.1 pad_maximum_fusion
  48.5 0.0 copy-done
  48.5 1.4 %fusion.24 = f32[16,1,384]{2,1,0:T(1,128)S(1)} fusion(f32[16,96,1]{1,2,0:T(1,128)S(1)} %bitcast.41, f32[16,96,384]{2,1,0:T(8,128)S(1)} %copy-done), kind=kOutput, calls=%fused_computation.39 | convolution fusion | flops 7077888 | bytes 2390016 | tf_op jit(solution)/shard_map/zkv,zk->zv/dot_general | solution.py:55
  49.9 0.0 copy-done.2
  49.9 0.0 copy-done.1
  49.9 2.6 %fusion.3 = f32[16,1,96]{2,1,0:T(1,128)S(1)} fusion(f32[16,96,384]{2,1,0:T(8,128)S(1)} %copy-done.1, f32[16,384,1]{1,0,2:T(8,128)S(1)} %fusion.2), kind=kOutput, calls=%fused_computation.9 | convolution fusion | flops 7077888 | bytes 2390016 | tf_op jit(solution)/shard_map/zkv,zv->zk/dot_general | solution.py:38
  52.5 0.1 slice.19
  52.6 14.0 %all_gather.7 = f32[128,48]{1,0:T(8,128)S(1)} all-gather(f32[16,48]{1,0:T(8,128)S(1)} %slice.19), channel_id=1, replica_groups=mesh['floor'=4,'zone'=8] {'zone'}, dimensions={0}, use_global_device_ids=true | all-gather | bytes 27648 | tf_op jit(solution)/shard_map/all_gather | solution.py:48
  66.6 0.8 multiply_add_fusion
  67.4 0.3 fusion.7
  67.6 13.9 %psum.30 = f32[4,48]{1,0:T(4,128)S(1)} all-reduce(f32[4,48]{1,0:T(4,128)S(1)} %fusion.7), channel_id=1, replica_groups=mesh['floor'=4,'zone'=8] {'zone'}, use_global_device_ids=true, to_apply=%region_3.0 | all-reduce | flops 192 | bytes 1536 | tf_op jit(solution)/shard_map/psum | solution.py:42
  81.5 7.9 %psum.31 = f32[4,48]{1,0:T(4,128)S(1)} all-reduce(f32[4,48]{1,0:T(4,128)S(1)} %psum.30), channel_id=1, replica_groups=mesh['floor'=4,'zone'=8] {'floor'}, use_global_device_ids=true, to_apply=%region_4.0 | all-reduce | flops 192 | bytes 1536 | tf_op jit(solution)/shard_map/psum | solution.py:43
  89.5 0.0 copy-start.7
  89.5 0.2 convolution_subtract_fusion
  89.7 0.1 pad_maximum_fusion.1
  89.8 1.4 %fusion.25 = f32[16,1,384]{2,1,0:T(1,128)S(1)} fusion(f32[16,96,1]{1,2,0:T(1,128)S(1)} %bitcast.42, f32[16,96,384]{2,1,0:T(8,128)S(1)} %copy-done), kind=kOutput, calls=%fused_computation.40 | convolution fusion | flops 7077888 | bytes 2390016 | tf_op jit(solution)/shard_map/zkv,zk->zv/dot_general | solution.py:55
  91.2 0.6 fusion
  91.8 0.0 copy-done.7
  (2 shorter events, 0.0 us)
Async XLA Ops:
  0.6 47.8 %copy-start = (f32[16,96,384]{2,1,0:T(8,128)S(1)}, f32[16,96,384]{2,1,0:T(8,128)}, u32[]{:S(2)}) copy-start(f32[16,96,384]{2,1,0:T(8,128)} %param.9) | copy-start | bytes 7077892
  0.6 20.3 %copy-start.3 = (f32[16,48]{1,0:T(8,128)S(1)}, f32[16,48]{1,0:T(8,128)}, u32[]{:S(2)}) copy-start(f32[16,48]{1,0:T(8,128)} %param.15) | copy-start | bytes 9220
  0.7 20.2 %copy-start.4 = (s32[16,4]{0,1:T(4,128)S(1)}, s32[16,4]{0,1:T(4,128)}, u32[]{:S(2)}) copy-start(s32[16,4]{0,1:T(4,128)} %param.16) | copy-start | bytes 772
  0.7 20.5 %copy-start.8 = (s32[16]{0:T(128)S(1)}, s32[16]{0:T(128)}, u32[]{:S(2)}) copy-start(s32[16]{0:T(128)} %param.17) | copy-start | bytes 196
  0.7 47.5 %copy-start.5 = (f32[4,48]{1,0:T(4,128)S(1)}, f32[4,48]{1,0:T(4,128)}, u32[]{:S(2)}) copy-start(f32[4,48]{1,0:T(4,128)} %param.14) | copy-start | bytes 2308
  0.7 47.5 %copy-start.6 = (f32[4,48]{1,0:T(4,128)S(1)}, f32[4,48]{1,0:T(4,128)}, u32[]{:S(2)}) copy-start(f32[4,48]{1,0:T(4,128)} %param.13) | copy-start | bytes 2308
  0.7 49.2 %copy-start.2 = (f32[16,384]{1,0:T(8,128)S(1)}, f32[16,384]{1,0:T(8,128)}, u32[]{:S(2)}) copy-start(f32[16,384]{1,0:T(8,128)} %param.11) | copy-start | bytes 73732
  48.2 1.7 %copy-start.1 = (f32[16,96,384]{2,1,0:T(8,128)S(1)}, f32[16,96,384]{2,1,0:T(8,128)}, u32[]{:S(2)}) copy-start(f32[16,96,384]{2,1,0:T(8,128)} %param.10) | copy-start | bytes 7077892
  89.5 2.3 %copy-start.7 = (f32[4,48]{1,0:T(4,128)}, f32[4,48]{1,0:T(4,128)S(1)}, u32[]{:S(2)}) copy-start(f32[4,48]{1,0:T(4,128)S(1)} %multiply_add_fusion.2) | copy-start | bytes 2308
where the time goes:
time: 92.1 us; the launch traced here: 91.8 us
  blocking collectives  78.3 us (85%)
  matrix products  11.7 us (13%)
    psum x2, blocking collectives, local(): floor_load = lax.psum(partial_load, 'zone')  30.8 us
    all_gather x2, blocking collectives, local(): floor_bound = lax.all_gather(bound, 'zone', axis=0, tiled=True)  29.7 us
    psum x2, blocking collectives, local(): total = lax.psum(floor_load, 'floor')  17.8 us
    dot_general x2, matrix products, local(): jnp.einsum('zkv,zv->zk', plant_map, control, precision=lax.Precision.HIGH...  7 us
    dot_general x2, matrix products, local(): jnp.einsum('zkv,zk->zv', factor, target, precision=lax.Precision.HIGHEST)  2.88 us

commit v1 on v0

--- a/solution.py
+++ b/solution.py
@@ -40,7 +40,9 @@
         bound = outputs[:, HORIZON:]
         partial_load = jnp.dot(onehot.T, shares, precision=lax.Precision.HIGHEST)
         floor_load = lax.psum(partial_load, "zone")
-        total = lax.psum(floor_load, "floor")
+        total = floor_load
+        for hop in (1, 2):
+            total = total + lax.ppermute(total, "floor", [(dev, dev ^ hop) for dev in range(4)])
         excess = (total - demand) * (LOOPS / zones_all)
         shift = jnp.dot(onehot, excess + price, precision=lax.Precision.HIGHEST)
         price = price + excess

time: 92.1 us -> 81.7 us (0.89)
  blocking collectives: 78.3 us -> 59.6 us
  starting transfers between devices: 0 us -> 5.17 us
  waiting for transfers between devices: 0 us -> 3.2 us
    psum x2 -> x0, blocking collectives: 17.8 us -> none  [local(): total = lax.psum(floor_load, 'floor')]
    ppermute x0 -> x4, starting transfers between devices: none -> 5.17 us  [local(): lax.ppermute(total, 'floor', [(dev, dev ^ hop) for dev in range(4)])]
    ppermute x0 -> x4, waiting for transfers between devices: none -> 3.2 us  [local(): lax.ppermute(total, 'floor', [(dev, dev ^ hop) for dev in range(4)])]
    all_gather x2, blocking collectives: 29.7 us -> 28 us  [local(): floor_bound = lax.all_gather(bound, 'zone', axis=0, tiled=True)]
  transfers between devices with their start and end apart: 0 -> 4, of which waited for: 0 -> 2; matrix products, arithmetic and copies ran while one was open for 0% -> 1% of each run, Pallas kernels for 0% -> 0%
where the time goes in v1:
time: 81.7 us; the launch traced here: 81.5 us
  blocking collectives  59.6 us (73%)
  matrix products  11.7 us (14%)
  starting transfers between devices  5.17 us (6%)
  waiting for transfers between devices  3.2 us (4%)
  other arithmetic  0.88 us (1%)
    psum x2, blocking collectives, local(): floor_load = lax.psum(partial_load, 'zone')  31.7 us
    all_gather x2, blocking collectives, local(): floor_bound = lax.all_gather(bound, 'zone', axis=0, tiled=True)  28 us
    dot_general x2, matrix products, local(): jnp.einsum('zkv,zv->zk', plant_map, control, precision=lax.Precision.HIGH...  7 us
    ppermute x4, starting transfers between devices, local(): lax.ppermute(total, 'floor', [(dev, dev ^ hop) for dev in range(4)])  5.17 us
    ppermute x4, waiting for transfers between devices, local(): lax.ppermute(total, 'floor', [(dev, dev ^ hop) for dev in range(4)])  3.2 us
    dot_general x2, matrix products, local(): jnp.einsum('zkv,zk->zv', factor, target, precision=lax.Precision.HIGHEST)  2.88 us
  transfers between devices with their start and end apart: 4, of which 2 were waited for; matrix products, arithmetic and copies ran while one was open for 1% of the time, Pallas kernels for 0%

profile of v1, /device:TPU:0, one launch (start us, length us, event | category | flops | bytes accessed | tf_op | source)
XLA Modules:
  0.0 81.5 jit_solution(13417583378962574427)
XLA Ops:
  0.6 0.0 copy-start
  0.6 0.0 copy-start.8
  0.7 0.0 copy-start.4
  0.7 0.0 copy-start.3
  0.7 0.0 copy-start.5
  0.7 0.0 copy-start.6
  0.7 0.0 copy-start.2
  0.7 4.4 %fusion.5 = f32[16,1,96]{2,1,0:T(1,128)S(1)} fusion(f32[16,96,384]{2,1,0:T(8,128)} %param.10, f32[16,384,1]{1,0,2:T(8,128)} %bitcast.43), kind=kOutput, calls=%fused_computation.11 | convolution fusion | flops 7077888 | bytes 2390016 | tf_op jit(solution)/shard_map/zkv,zv->zk/dot_general | solution.py:38
  5.1 0.0 copy-done.8
  5.1 0.3 fusion.8
  5.4 18.1 %psum.14 = f32[4,48]{1,0:T(4,128)S(1)} all-reduce(f32[4,48]{1,0:T(4,128)S(1)} %fusion.8), channel_id=1, replica_groups=mesh['floor'=4,'zone'=8] {'zone'}, use_global_device_ids=true, to_apply=%region_0.0 | all-reduce | flops 192 | bytes 1536 | tf_op jit(solution)/shard_map/psum | solution.py:42
  23.5 0.0 copy-start.1
  23.5 1.5 %collective-permute-start = (f32[4,48]{1,0:T(4,128)S(1)}, f32[4,48]{1,0:T(4,128)S(1)}, u32[]{:S(2)}, u32[]{:S(2)}) collective-permute-start(f32[4,48]{1,0:T(4,128)S(1)} %psum.14), channel_id=1, source_target_pairs={{0,8},{8,0},{16,24},{24,16},{1,9},{9,1},{17,25},{25,17},{2,10},{10... | collective-permute-start | bytes 2312 | tf_op jit(solution)/shard_map/ppermute | solution.py:45
  25.0 0.1 slice.17
  25.1 0.0 copy-done.4
  25.1 0.1 convert_reduce_fusion
  25.2 14.0 %all_gather.6 = f32[128,48]{1,0:T(8,128)S(1)} all-gather(f32[16,48]{1,0:T(8,128)S(1)} %slice.17), channel_id=1, replica_groups=mesh['floor'=4,'zone'=8] {'zone'}, dimensions={0}, use_global_device_ids=true | all-gather | bytes 27648 | tf_op jit(solution)/shard_map/all_gather | solution.py:50
  39.2 0.0 collective-permute-done
  39.2 1.5 %collective-permute-start.1 = (f32[4,48]{1,0:T(4,128)S(1)}, f32[4,48]{1,0:T(4,128)S(1)}, u32[]{:S(2)}, u32[]{:S(2)}) collective-permute-start(f32[4,48]{1,0:T(4,128)S(1)} %add.36), channel_id=1, source_target_pairs={{0,16},{8,24},{16,0},{24,8},{1,17},{9,25},{17,1},{25,9},{2,18},{10... | collective-permute-start | bytes 2312 | tf_op jit(solution)/shard_map/ppermute | solution.py:45
  40.7 0.0 copy-done.3
  40.7 0.2 multiply_subtract_fusion.1
  40.8 1.9 %collective-permute-done.1 = f32[4,48]{1,0:T(4,128)S(1)} collective-permute-done((f32[4,48]{1,0:T(4,128)S(1)}, f32[4,48]{1,0:T(4,128)S(1)}, u32[]{:S(2)}, u32[]{:S(2)}) %collective-permute-start.1) | collective-permute-done | bytes 800 | tf_op jit(solution)/shard_map/ppermute | solution.py:45
  42.7 0.0 copy-done.5
  42.7 0.0 copy-done.6
  42.8 0.2 convolution_subtract_fusion.1
  42.9 0.1 pad_maximum_fusion
  43.0 0.0 copy-done
  43.0 1.4 %fusion.23 = f32[16,1,384]{2,1,0:T(1,128)S(1)} fusion(f32[16,96,1]{1,2,0:T(1,128)S(1)} %bitcast.41, f32[16,96,384]{2,1,0:T(8,128)S(1)} %copy-done), kind=kOutput, calls=%fused_computation.38 | convolution fusion | flops 7077888 | bytes 2390016 | tf_op jit(solution)/shard_map/zkv,zk->zv/dot_general | solution.py:57
  44.5 0.0 copy-done.2
  44.5 0.0 copy-done.1
  44.5 2.6 %fusion.3 = f32[16,1,96]{2,1,0:T(1,128)S(1)} fusion(f32[16,96,384]{2,1,0:T(8,128)S(1)} %copy-done.1, f32[16,384,1]{1,0,2:T(8,128)S(1)} %fusion.2), kind=kOutput, calls=%fused_computation.9 | convolution fusion | flops 7077888 | bytes 2390016 | tf_op jit(solution)/shard_map/zkv,zv->zk/dot_general | solution.py:38
  47.1 0.1 slice.19
  47.2 0.3 fusion.7
  47.4 13.6 %psum.15 = f32[4,48]{1,0:T(4,128)S(1)} all-reduce(f32[4,48]{1,0:T(4,128)S(1)} %fusion.7), channel_id=1, replica_groups=mesh['floor'=4,'zone'=8] {'zone'}, use_global_device_ids=true, to_apply=%region_2.0 | all-reduce | flops 192 | bytes 1536 | tf_op jit(solution)/shard_map/psum | solution.py:42
  61.0 0.6 collective-permute-start.2
  61.6 14.0 %all_gather.7 = f32[128,48]{1,0:T(8,128)S(1)} all-gather(f32[16,48]{1,0:T(8,128)S(1)} %slice.19), channel_id=1, replica_groups=mesh['floor'=4,'zone'=8] {'zone'}, dimensions={0}, use_global_device_ids=true | all-gather | bytes 27648 | tf_op jit(solution)/shard_map/all_gather | solution.py:50
  75.6 0.0 collective-permute-done.2
  75.6 1.5 %collective-permute-start.3 = (f32[4,48]{1,0:T(4,128)S(1)}, f32[4,48]{1,0:T(4,128)S(1)}, u32[]{:S(2)}, u32[]{:S(2)}) collective-permute-start(f32[4,48]{1,0:T(4,128)S(1)} %add.40), channel_id=1, source_target_pairs={{0,16},{8,24},{16,0},{24,8},{1,17},{9,25},{17,1},{25,9},{2,18},{10... | collective-permute-start | bytes 2312 | tf_op jit(solution)/shard_map/ppermute | solution.py:45
  77.1 0.8 multiply_add_fusion
  77.9 1.3 %collective-permute-done.3 = f32[4,48]{1,0:T(4,128)S(1)} collective-permute-done((f32[4,48]{1,0:T(4,128)S(1)}, f32[4,48]{1,0:T(4,128)S(1)}, u32[]{:S(2)}, u32[]{:S(2)}) %collective-permute-start.3) | collective-permute-done | bytes 800 | tf_op jit(solution)/shard_map/ppermute | solution.py:45
  79.2 0.0 copy-start.7
  79.2 0.2 convolution_subtract_fusion
  79.4 0.1 pad_maximum_fusion.1
  79.5 1.4 %fusion.24 = f32[16,1,384]{2,1,0:T(1,128)S(1)} fusion(f32[16,96,1]{1,2,0:T(1,128)S(1)} %bitcast.42, f32[16,96,384]{2,1,0:T(8,128)S(1)} %copy-done), kind=kOutput, calls=%fused_computation.39 | convolution fusion | flops 7077888 | bytes 2390016 | tf_op jit(solution)/shard_map/zkv,zk->zv/dot_general | solution.py:57
  80.9 0.6 fusion
  81.5 0.0 copy-done.7
  (4 shorter events, 0.0 us)
Async XLA Ops:
  0.6 42.4 %copy-start = (f32[16,96,384]{2,1,0:T(8,128)S(1)}, f32[16,96,384]{2,1,0:T(8,128)}, u32[]{:S(2)}) copy-start(f32[16,96,384]{2,1,0:T(8,128)} %param.9) | copy-start | bytes 7077892
  0.6 4.5 %copy-start.8 = (s32[16]{0:T(128)S(1)}, s32[16]{0:T(128)}, u32[]{:S(2)}) copy-start(s32[16]{0:T(128)} %param.17) | copy-start | bytes 196
  0.7 24.4 %copy-start.4 = (s32[16,4]{0,1:T(4,128)S(1)}, s32[16,4]{0,1:T(4,128)}, u32[]{:S(2)}) copy-start(s32[16,4]{0,1:T(4,128)} %param.16) | copy-start | bytes 772
  0.7 40.0 %copy-start.3 = (f32[16,48]{1,0:T(8,128)S(1)}, f32[16,48]{1,0:T(8,128)}, u32[]{:S(2)}) copy-start(f32[16,48]{1,0:T(8,128)} %param.15) | copy-start | bytes 9220
  0.7 42.1 %copy-start.5 = (f32[4,48]{1,0:T(4,128)S(1)}, f32[4,48]{1,0:T(4,128)}, u32[]{:S(2)}) copy-start(f32[4,48]{1,0:T(4,128)} %param.14) | copy-start | bytes 2308
  0.7 42.1 %copy-start.6 = (f32[4,48]{1,0:T(4,128)S(1)}, f32[4,48]{1,0:T(4,128)}, u32[]{:S(2)}) copy-start(f32[4,48]{1,0:T(4,128)} %param.13) | copy-start | bytes 2308
  0.7 43.8 %copy-start.2 = (f32[16,384]{1,0:T(8,128)S(1)}, f32[16,384]{1,0:T(8,128)}, u32[]{:S(2)}) copy-start(f32[16,384]{1,0:T(8,128)} %param.11) | copy-start | bytes 73732
  23.5 21.0 %copy-start.1 = (f32[16,96,384]{2,1,0:T(8,128)S(1)}, f32[16,96,384]{2,1,0:T(8,128)}, u32[]{:S(2)}) copy-start(f32[16,96,384]{2,1,0:T(8,128)} %param.10) | copy-start | bytes 7077892
  23.5 15.7 %collective-permute-start = (f32[4,48]{1,0:T(4,128)S(1)}, f32[4,48]{1,0:T(4,128)S(1)}, u32[]{:S(2)}, u32[]{:S(2)}) collective-permute-start(f32[4,48]{1,0:T(4,128)S(1)} %psum.14), channel_id=1, source_target_pairs={{0,8},{8,0},{16,24},{24,16},{1,9},{9,1},{17,25},{25,17},{2,10},{10... | collective-permute-start | bytes 2312 | tf_op jit(solution)/shard_map/ppermute | solution.py:45
  39.2 3.6 %collective-permute-start.1 = (f32[4,48]{1,0:T(4,128)S(1)}, f32[4,48]{1,0:T(4,128)S(1)}, u32[]{:S(2)}, u32[]{:S(2)}) collective-permute-start(f32[4,48]{1,0:T(4,128)S(1)} %add.36), channel_id=1, source_target_pairs={{0,16},{8,24},{16,0},{24,8},{1,17},{9,25},{17,1},{25,9},{2,18},{10... | collective-permute-start | bytes 2312 | tf_op jit(solution)/shard_map/ppermute | solution.py:45
  61.0 14.6 %collective-permute-start.2 = (f32[4,48]{1,0:T(4,128)S(1)}, f32[4,48]{1,0:T(4,128)S(1)}, u32[]{:S(2)}, u32[]{:S(2)}) collective-permute-start(f32[4,48]{1,0:T(4,128)S(1)} %psum.15), channel_id=1, source_target_pairs={{0,8},{8,0},{16,24},{24,16},{1,9},{9,1},{17,25},{25,17},{2,10},{10... | collective-permute-start | bytes 2312 | tf_op jit(solution)/shard_map/ppermute | solution.py:45
  75.6 3.6 %collective-permute-start.3 = (f32[4,48]{1,0:T(4,128)S(1)}, f32[4,48]{1,0:T(4,128)S(1)}, u32[]{:S(2)}, u32[]{:S(2)}) collective-permute-start(f32[4,48]{1,0:T(4,128)S(1)} %add.40), channel_id=1, source_target_pairs={{0,16},{8,24},{16,0},{24,8},{1,17},{9,25},{17,1},{25,9},{2,18},{10... | collective-permute-start | bytes 2312 | tf_op jit(solution)/shard_map/ppermute | solution.py:45
  79.2 2.3 %copy-start.7 = (f32[4,48]{1,0:T(4,128)}, f32[4,48]{1,0:T(4,128)S(1)}, u32[]{:S(2)}) copy-start(f32[4,48]{1,0:T(4,128)S(1)} %multiply_add_fusion.2) | copy-start | bytes 2308
